TPU v7x, 128 devices: a whole 4x4x4 slice. The times are simulated.
128 devices in a mesh: seq: 8 (over x, core), tp: 16 (over y, z).
Axes of the slice: x: 4, y: 4, z: 4, core: 2. Of those that a mesh axis runs over, the one named last changes fastest.
Arguments:
- vit_input: bfloat16 [8192, 1280], P(('seq', 'tp')), may hold values from -6 to 6
- image_lengths: int32 [8, 2], P('seq'), may hold values from 1 to 192, 256 in all within a row
- positions: int32 [2048], replicated, may hold values from 0 to 2047, each once
- vit_ln_gain: float32 [1280], replicated, may hold values from 0.25 to 1.75
- w_qkv: bfloat16 [1280, 3, 1280], P(None, None, 'tp'), may hold values from -0.15625 to 0.15625
- w_proj: bfloat16 [1280, 1280], P('tp'), may hold values from -0.15625 to 0.15625
- merger_ln_gain: float32 [1280], replicated, may hold values from 0.25 to 1.75
- merger_w1: bfloat16 [5120, 5120], P(None, 'tp'), may hold values from -0.078125 to 0.078125
- merger_w2: bfloat16 [5120, 8192], P('tp'), may hold values from -0.36336105 to 0.36336105
- norm_gain: float32 [8192], P('seq'), may hold values from 0.25 to 1.75
- gate_up_weight: bfloat16 [8192, 2, 29568], P('seq', None, 'tp'), may hold values from -0.0625 to 0.0625
- down_weight: bfloat16 [29568, 8192], P('tp', 'seq'), may hold values from -0.125 to 0.125
Outputs:
- mixed: bfloat16 [2048, 8192], P('tp', 'seq')
Inputs may be any that keep to these rules, and one draw needn't show every extreme that they name: `image_lengths`: each row sums to 256. `positions`: a permutation: every slot once.
All inputs are finite; a program needn't handle non-finite values.
Results may differ from a plain program's by a relative error of at most 0.038.
Values may be sent and summed in bfloat16 or wider, within the bound.
A program may use at most 128 MiB of HBM per device.

v0:
```python
import jax
import jax.numpy as jnp
from jax import lax
from jax.experimental import pallas as pl
from jax.experimental.pallas import tpu as pltpu
from jax.sharding import Mesh
from jax.sharding import PartitionSpec as P

D = 8192
HD = 80
TP = ("tp_0", "tp_1")
SEQ_TP = ("seq", "tp_0", "tp_1")

MESH_ID = pl.DeviceIdType.MESH
AXES = ("tp_0", "tp_1")


def ring(axis, step):
    return {axis: lax.rem(lax.axis_index(axis) + step, 4)}


def remote(src, dst, send, recv, target):
    return pltpu.make_async_remote_copy(
        src_ref=src, dst_ref=dst, send_sem=send, recv_sem=recv, device_id=target, device_id_type=MESH_ID
    )


def greet(targets):
    barrier = pltpu.get_barrier_semaphore()
    for target in targets:
        pl.semaphore_signal(barrier, inc=1, device_id=target, device_id_type=MESH_ID)
    pl.semaphore_wait(barrier, len(targets))


def plane_neighbours():
    return [ring(axis, step) for axis in AXES for step in (1, 3)]


def gather_plane(own, slot, half_cut, quarter_cut, send, recv, forward=None):
    here = [lax.axis_index(axis) for axis in AXES]
    sent = []

    def index(half, first, second):
        offsets = (first, second) if half == 0 else (second, first)
        spots = [lax.rem(at + off, 4) for at, off in zip(here, offsets)]
        return spots[0] * 4 + spots[1]

    def place(half, first, second):
        return slot(index(half, first, second))

    def source(half, first, second):
        return own if (first, second) == (0, 0) else place(half, first, second)

    def start(half, phase, kind, axis, step, first, second, cut):
        at = half * 20 + phase * 4 + kind
        copy = remote(
            cut(source(half, first, second)), cut(place(half, first, second)), send.at[at], recv.at[at], ring(axis, step)
        )
        copy.start()
        sent.append(copy)

    def landed(half, phase, kind, axis, first, second, cut):
        at = half * 20 + phase * 4 + kind
        target = cut(place(half, first, second))
        remote(target, target, send.at[at], recv.at[at], ring(axis, 1)).wait_recv()
        if forward is not None:
            forward(at, lambda base: cut(base(index(half, first, second))))

    def axes(half):
        return (AXES[0], AXES[1]) if half == 0 else (AXES[1], AXES[0])

    def cuts(half):
        return (
            lambda ref: half_cut(ref, half),
            lambda ref: quarter_cut(ref, 2 * half),
            lambda ref: quarter_cut(ref, 2 * half + 1),
        )

    def spread(half, phase, first):
        whole, _, _ = cuts(half)
        axis = axes(half)[1]
        start(half, phase, 0, axis, 1, first, 0, whole)
        start(half, phase, 1, axis, 3, first, 0, whole)

    def relay(half, phase, first):
        whole, low, high = cuts(half)
        axis = axes(half)[1]
        landed(half, phase, 0, axis, first, 3, whole)
        start(half, phase, 2, axis, 1, first, 3, low)
        landed(half, phase, 1, axis, first, 1, whole)
        start(half, phase, 3, axis, 3, first, 1, high)

    def finish(half, phase, first):
        whole, low, high = cuts(half)
        axis = axes(half)[1]
        landed(half, phase, 2, axis, first, 2, low)
        landed(half, phase, 3, axis, first, 2, high)

    for half in (0, 1):
        whole, _, _ = cuts(half)
        start(half, 0, 0, axes(half)[0], 1, 0, 0, whole)
        start(half, 0, 1, axes(half)[0], 3, 0, 0, whole)
    for half in (0, 1):
        spread(half, 1, 0)
    yield
    for half in (0, 1):
        whole, low, high = cuts(half)
        axis = axes(half)[0]
        landed(half, 0, 0, axis, 3, 0, whole)
        start(half, 0, 2, axis, 1, 3, 0, low)
        spread(half, 2, 3)
        landed(half, 0, 1, axis, 1, 0, whole)
        start(half, 0, 3, axis, 3, 1, 0, high)
        spread(half, 3, 1)
    yield
    for half in (0, 1):
        relay(half, 1, 0)
    yield
    for half in (0, 1):
        whole, low, high = cuts(half)
        axis = axes(half)[0]
        landed(half, 0, 2, axis, 2, 0, low)
        landed(half, 0, 3, axis, 2, 0, high)
        spread(half, 4, 2)
    yield
    for phase, first in ((2, 3), (3, 1), (4, 2)):
        for half in (0, 1):
            relay(half, phase, first)
    yield
    for phase, first in ((1, 0), (2, 3), (3, 1), (4, 2)):
        for half in (0, 1):
            finish(half, phase, first)
    for copy in sent:
        copy.wait_send()


def reduce_plane(term, got, made, sums, send, recv, emit, eager=True):
    here = [lax.axis_index(axis) for axis in AXES]
    sent = []

    def axes(half):
        return (AXES[1], AXES[0]) if half == 0 else (AXES[0], AXES[1])

    def part(half, first, second, which):
        offsets = (first, second) if half == 0 else (second, first)
        spots = [lax.rem(at + off, 4) for at, off in zip(here, offsets)]
        return term(spots[0] * 4 + spots[1], 2 * half + which)

    def phase_source(half, phase):
        if phase < 4:
            return lambda offset, which: part(half, phase, offset, which)
        return lambda offset, which: sums.at[half * 8 + offset * 2 + which]

    def slot(half, phase, kind):
        return half * 30 + phase * 6 + kind

    def start(half, phase, kind, src, step):
        axis = axes(half)[0 if phase < 4 else 1]
        at = slot(half, phase, kind)
        copy = remote(src, got.at[at], send.at[at], recv.at[at], ring(axis, step))
        copy.start()
        sent.append(copy)

    def landed(half, phase, kind):
        at = slot(half, phase, kind)
        axis = axes(half)[0 if phase < 4 else 1]
        remote(got.at[at], got.at[at], send.at[at], recv.at[at], ring(axis, 1)).wait_recv()
        return got[at].astype(jnp.float32)

    def raw(half, phase):
        own = phase_source(half, phase)
        start(half, phase, 0, own(2, 0), 1)
        start(half, phase, 3, own(2, 1), 3)
        start(half, phase, 1, own(1, 1), 1)
        start(half, phase, 4, own(3, 0), 3)

    def summed(half, phase):
        own = phase_source(half, phase)
        for kind, offset, which, step in ((0, 1, 0, 1), (3, 3, 1, 3)):
            at = half * 10 + phase * 2 + which
            made[at] = (own(offset, which)[...].astype(jnp.float32) + landed(half, phase, kind)).astype(made.dtype)
            start(half, phase, kind + 2, made.at[at], step)

    def total(half, phase):
        own = phase_source(half, phase)
        return [
            own(0, which)[...].astype(jnp.float32) + landed(half, phase, near) + landed(half, phase, far)
            for which, near, far in ((0, 4, 2), (1, 1, 5))
        ]

    def settle(half, phase):
        for which, value in enumerate(total(half, phase)):
            sums[half * 8 + phase * 2 + which] = value.astype(sums.dtype)

    order = (2, 1, 3, 0)
    both = (0, 1)

    def late(first):
        own = phase_source_of_last
        for half in both:
            source = own(half)
            if first == 2:
                start(half, 4, 0, source(2, 0), 1)
                start(half, 4, 3, source(2, 1), 3)
            if first == 1:
                start(half, 4, 1, source(1, 1), 1)
            if first == 3:
                start(half, 4, 4, source(3, 0), 3)

    def phase_source_of_last(half):
        return phase_source(half, 4)

    for half in both:
        raw(half, order[0])
    for half in both:
        raw(half, order[1])
    if not eager:
        for phase in order[2:]:
            for half in both:
                raw(half, phase)
    yield
    for at, phase in enumerate(order):
        for half in both:
            summed(half, phase)
        if eager and at + 2 < 4:
            for half in both:
                raw(half, order[at + 2])
        if eager and at >= 1:
            for half in both:
                settle(half, order[at - 1])
            late(order[at - 1])
    yield
    if not eager:
        for phase in order[:3]:
            for half in both:
                settle(half, phase)
            late(phase)
    yield
    for half in both:
        summed(half, 4)
    yield
    for half in both:
        settle(half, 0)
    for half in both:
        for which, value in enumerate(total(half, 4)):
            emit(2 * half + which, value)
    for copy in sent:
        copy.wait_send()


def run(steps):
    for _ in steps:
        pass
WIDE = 2176
PADDED = 1920


def along_x(step):
    seq = lax.axis_index("seq")
    return {"seq": lax.rem(seq + 2 * step, 8)}


def partner():
    seq = lax.axis_index("seq")
    return {"seq": seq + 1 - 2 * lax.rem(seq, 2)}


ROW_CUTS = ((0, 32), (32, 16), (48, 16), (64, 16))
ROW_HALVES = ((0, 48), (48, 32))


def share_with_partner(buffer, core, send, recv, sent, expected):
    def forward(at, view):
        piece = view(lambda t: buffer(core, t))
        copy = remote(piece, piece, send.at[at], recv.at[at], partner())
        copy.start()
        sent.append(copy)
        other = view(lambda t: buffer(1 - core, t))
        expected.append(remote(other, other, send.at[at], recv.at[at], partner()))

    return forward


def norm_rows(values, gain):
    mean = jnp.mean(values, axis=-1, keepdims=True)
    centered = values - mean
    variance = jnp.mean(centered * centered, axis=-1, keepdims=True)
    return centered * lax.rsqrt(variance + 1e-06) * gain


def vision_kernel(
    vit, ends, ln_gain, merger_gain, w_qkv, w_proj, w_one, w_two, out,
    own, patches, qkv, wq, wp, att, heads, lined, tiles, block_in, merged, one, expanded, two, terms,
    got, made, sums, parcels, block,
    wsem, asend, arecv, psend, precv, qsend, qrecv, hsend, hrecv, msend, mrecv,
    send, recv, xsend, xrecv, gsend, grecv, dsend, drecv,
):
    seq = lax.axis_index("seq")
    x, core = seq // 2, lax.rem(seq, 2)
    y, z = [lax.axis_index(axis) for axis in AXES]
    me = y * 4 + z
    others = [(dy, dz) for dy in range(4) for dz in range(4) if (dy, dz) != (0, 0)]

    def peer(dy, dz):
        return {"tp_0": lax.rem(y + dy, 4), "tp_1": lax.rem(z + dz, 4)}

    def peer_index(dy, dz):
        return lax.rem(y + dy, 4) * 4 + lax.rem(z + dz, 4)

    def proj_slot(side, t):
        return wp.at[t, :, pl.ds(pl.multiple_of(side * 640, 128), 640)]

    wq[:, pl.ds(80, 48), :] = jnp.zeros((3, 48, 1280), jnp.bfloat16)
    loads = [
        pltpu.make_async_copy(w_qkv, wq.at[:, pl.ds(0, 80), :], wsem.at[0]),
        pltpu.make_async_copy(w_proj, wp.at[me], wsem.at[1]),
        pltpu.make_async_copy(w_one, one, wsem.at[2]),
        pltpu.make_async_copy(w_two, two, wsem.at[3]),
    ]
    for copy in loads:
        copy.start()
    targets = [peer(*offset) for offset in others] + [along_x(step) for step in (1, 2, 3)] + [partner()]
    barrier = pltpu.get_barrier_semaphore()
    for target in targets:
        pl.semaphore_signal(barrier, inc=1, device_id=target, device_id_type=MESH_ID)
    own[...] = norm_rows(vit[...].astype(jnp.float32), ln_gain[...]).astype(jnp.bfloat16)
    pl.semaphore_wait(barrier, len(targets))

    rows_half = lambda ref, half: ref.at[pl.ds(half * 32, 32), :]
    rows_quarter = lambda ref, at: ref.at[pl.ds(at * 16, 16), :]
    patches[me] = own[...]
    run(gather_plane(own, lambda t: patches.at[t], rows_half, rows_quarter, asend, arecv))

    loads[1].wait()
    shared, awaited = [], []
    weights = gather_plane(
        proj_slot(core, me),
        lambda t: proj_slot(core, t),
        lambda ref, half: ref.at[pl.ds(*ROW_HALVES[half]), :],
        lambda ref, at: ref.at[pl.ds(*ROW_CUTS[at]), :],
        psend,
        precv,
        share_with_partner(proj_slot, core, qsend, qrecv, shared, awaited),
    )
    next(weights)
    loads[0].wait()

    @pl.loop(0, 4)
    def _(n):
        rows = pl.ds(pl.multiple_of(n * 256, 256), 256)
        some = patches[pl.ds(n * 4, 4)].reshape(256, 1280)
        for which in range(3):
            qkv[which, rows, :] = lax.dot_general(
                some, wq[which], (((1,), (1,)), ((), ())), preferred_element_type=jnp.float32
            ).astype(jnp.bfloat16)

    next(weights)
    end = ends[0:1, 0:1]

    def attend_rows(n):
        rows = pl.ds(pl.multiple_of(n * 256, 256), 256)
        scores = lax.dot_general(
            qkv[0, rows, :], qkv[1], (((1,), (1,)), ((), ())), preferred_element_type=jnp.float32
        ) * HD ** (-0.5)
        query_first = n * 256 + lax.broadcasted_iota(jnp.int32, (256, 1), 0) < end
        key_first = lax.broadcasted_iota(jnp.int32, (1, 1024), 1) < end
        query_first = jnp.where(query_first, 1, 0)
        key_first = jnp.where(key_first, 1, 0)
        scores = jnp.where(query_first == key_first, scores, -1e30)
        top = jnp.max(scores, axis=-1, keepdims=True)
        expo = jnp.exp(scores - top)
        share = (expo / jnp.sum(expo, axis=-1, keepdims=True)).astype(jnp.bfloat16)
        mixed = jnp.dot(share, qkv[2], preferred_element_type=jnp.float32).astype(jnp.bfloat16)
        att[pl.ds(n * 4, 4)] = mixed.reshape(4, 64, 128)

    for n in range(2):
        @pl.loop(2 * n, 2 * n + 2)
        def _(at):
            attend_rows(at)

        next(weights)
    sent = []
    for at, offset in enumerate(others):
        copy = remote(att.at[peer_index(*offset)], heads.at[me], hsend.at[at], hrecv.at[at], peer(*offset))
        copy.start()
        sent.append(copy)
    heads[me] = att[me]
    next(weights)
    run(weights)
    for copy in shared:
        copy.wait_send()
    for copy in awaited:
        copy.wait_recv()
    for at, (dy, dz) in enumerate(others):
        landing = heads.at[peer_index(4 - dy, 4 - dz)]
        remote(landing, landing, hsend.at[at], hrecv.at[at], peer(dy, dz)).wait_recv()
    for copy in sent:
        copy.wait_send()
    lined[...] = vit[...].astype(jnp.float32)

    @pl.loop(0, 16)
    def _(head):
        lined[...] += jnp.dot(heads[head, :, :80], wp[head], preferred_element_type=jnp.float32)

    ready = norm_rows(lined[...], merger_gain[...])
    for tile in range(10):
        tiles[tile] = ready[:, tile * 128 : tile * 128 + 128]
    for at in range(4):
        for tile in range(10):
            strided = tiles[tile, pl.ds(at, 16, stride=4), :]
            block_in[:, pl.ds(at * 1280 + tile * 128, 128)] = strided.astype(jnp.bfloat16)
    merged[pl.ds(pl.multiple_of(me * 16, 16), 16), :] = block_in[...]
    run(gather_plane(
        block_in,
        lambda t: merged.at[pl.ds(pl.multiple_of(t * 16, 16), 16), :],
        lambda ref, half: ref.at[:, pl.ds(half * 2560, 2560)],
        lambda ref, at: ref.at[:, pl.ds(at * 1280, 1280)],
        msend,
        mrecv,
    ))
    loads[2].wait()
    total = lax.dot_general(
        merged[...], one[...], (((1,), (1,)), ((), ())), preferred_element_type=jnp.float32
    )
    expanded[...] = (0.5 * total * (1.0 + lax.erf(total * (0.5 ** 0.5)))).astype(jnp.bfloat16)
    loads[3].wait()

    @pl.loop(0, 16)
    def _(n):
        columns = pl.ds(pl.multiple_of(n * 512, 512), 512)
        terms[:, columns] = jnp.dot(
            expanded[...], two[:, columns], preferred_element_type=jnp.float32
        ).astype(jnp.bfloat16)

    def emit(at, value):
        parcels[at, :, :2048] = value.astype(jnp.bfloat16)

    def term(t, at):
        return terms.at[pl.ds(pl.multiple_of(t * 16, 16), 16), pl.ds(at * 2048, 2048)]

    run(reduce_plane(term, got, made, sums, send, recv, emit))
    squares = jnp.zeros((16, 1), jnp.float32)
    for at in range(4):
        values = parcels[at, :, :2048].astype(jnp.float32)
        squares = squares + jnp.sum(values * values, axis=1, keepdims=True)
    high = squares.astype(jnp.bfloat16).astype(jnp.float32)
    low = squares - high
    lane = lax.broadcasted_iota(jnp.int32, (16, 128), 1)
    tail = jnp.where(lane == 0, high, jnp.where(lane == 1, low, 0.0)).astype(jnp.bfloat16)
    for at in range(4):
        parcels[at, :, 2048:] = tail
    mine = pl.ds(pl.multiple_of(x * 16, 16), 16)
    sent = []
    for step in (2, 1, 3):
        copy = remote(
            parcels.at[lax.rem(x + step, 4)], block.at[mine, :], xsend.at[step], xrecv.at[step], along_x(step)
        )
        copy.start()
        sent.append(copy)
    block[mine, :] = parcels[x]
    for step in (1, 3, 2):
        rows = pl.ds(pl.multiple_of(lax.rem(x + 4 - step, 4) * 16, 16), 16)
        landing = block.at[rows, :]
        remote(landing, landing, xsend.at[step], xrecv.at[step], along_x(step)).wait_recv()
    for copy in sent:
        copy.wait_send()
    forwarded, expected = [], []
    own_copy = remote(block, out.at[core, me], dsend.at[40], drecv.at[40], partner())
    own_copy.start()
    out[core, me] = block[...]
    run(gather_plane(
        block,
        lambda t: out.at[core, t],
        rows_half,
        rows_quarter,
        gsend,
        grecv,
        share_with_partner(lambda side, t: out.at[side, t], core, dsend, drecv, forwarded, expected),
    ))
    other = out.at[1 - core, me]
    expected.append(remote(other, other, dsend.at[40], drecv.at[40], partner()))
    own_copy.wait_send()
    for copy in forwarded:
        copy.wait_send()
    for copy in expected:
        copy.wait_recv()


def vision(vit, ends, ln_gain, merger_gain, w_qkv, w_proj, w_one, w_two, collective_id):
    anywhere = pl.BlockSpec(memory_space=pl.ANY)
    vmem = pl.BlockSpec(memory_space=pltpu.VMEM)
    dma = pltpu.SemaphoreType.DMA
    bf16 = jnp.bfloat16
    return pl.pallas_call(
        vision_kernel,
        out_shape=jax.ShapeDtypeStruct((2, 16, 64, WIDE), bf16),
        in_specs=[vmem] * 4 + [anywhere] * 4,
        out_specs=vmem,
        scratch_shapes=[
            pltpu.VMEM((64, 1280), bf16),
            pltpu.VMEM((16, 64, 1280), bf16),
            pltpu.VMEM((3, 1024, 128), bf16),
            pltpu.VMEM((3, 128, 1280), bf16),
            pltpu.VMEM((16, 80, 1280), bf16),
            pltpu.VMEM((16, 64, 128), bf16),
            pltpu.VMEM((16, 64, 128), bf16),
            pltpu.VMEM((64, 1280), jnp.float32),
            pltpu.VMEM((10, 64, 128), jnp.float32),
            pltpu.VMEM((16, 5120), bf16),
            pltpu.VMEM((256, 5120), bf16),
            pltpu.VMEM((320, 5120), bf16),
            pltpu.VMEM((256, 320), bf16),
            pltpu.VMEM((320, 8192), bf16),
            pltpu.VMEM((256, 8192), bf16),
            pltpu.VMEM((60, 16, 2048), bf16),
            pltpu.VMEM((20, 16, 2048), bf16),
            pltpu.VMEM((16, 16, 2048), bf16),
            pltpu.VMEM((4, 16, WIDE), bf16),
            pltpu.VMEM((64, WIDE), bf16),
            dma((4,)),
            dma((40,)), dma((40,)),
            dma((40,)), dma((40,)),
            dma((40,)), dma((40,)),
            dma((15,)), dma((15,)),
            dma((40,)), dma((40,)),
            dma((60,)), dma((60,)),
            dma((4,)), dma((4,)),
            dma((40,)), dma((40,)),
            dma((41,)), dma((41,)),
        ],
        compiler_params=pltpu.CompilerParams(
            collective_id=collective_id, has_side_effects=True, vmem_limit_bytes=56 * 1024 * 1024
        ),
        name="vision",
    )(vit, ends, ln_gain, merger_gain, w_qkv, w_proj, w_one, w_two)


GROUPS = ((0, 1024), (1024, 896))
BLOCKS = (((0, 0), (0, 1)), ((1, 1), (3, 0)), ((2, 0), (2, 1)), ((1, 0), (3, 1)))


def feed_forward_kernel(
    everyone, slots, gain, w_own, w_other, d_own, d_other, out,
    weights, downs, picks, raw, rows, strip, parts, came, hidden, got, made, sums, fin,
    wsem, osem, psend, precv, hsend, hrecv, send, recv, fsend, frecv,
):
    seq = lax.axis_index("seq")
    x, core = seq // 2, lax.rem(seq, 2)
    me = lax.axis_index("tp_0") * 4 + lax.axis_index("tp_1")
    real = w_own.shape[1]
    weights[:, pl.ds(1840, 80), :] = jnp.zeros((2, 80, 2048), jnp.bfloat16)
    downs[pl.ds(1840, 80), :] = jnp.zeros((80, 2048), jnp.bfloat16)
    sides = ((w_own, d_own, core), (w_other, d_other, 1 - core))

    def weight_copies(n):
        size = 256 if n < 7 else real - 1792
        return [
            pltpu.make_async_copy(
                w.at[:, pl.ds(n * 256, size), :],
                weights.at[:, pl.ds(n * 256, size), pl.ds(pl.multiple_of(at * 1024, 1024), 1024)],
                wsem.at[n, side],
            )
            for side, (w, _, at) in enumerate(sides)
        ]

    def down_copies():
        return [
            pltpu.make_async_copy(
                d, downs.at[pl.ds(0, real), pl.ds(pl.multiple_of(at * 1024, 1024), 1024)], osem.at[side]
            )
            for side, (_, d, at) in enumerate(sides)
        ]

    for n in range(8):
        for copy in weight_copies(n):
            copy.start()
    for copy in down_copies():
        copy.start()
    strip[...] = jnp.zeros_like(strip)

    def owner(step):
        return lax.rem(x + step, 4)

    def pick(block):
        upper, lower = BLOCKS[block]
        row = lax.broadcasted_iota(jnp.int32, (256, 1), 0)
        top = row < 128
        at = jnp.where(top, owner(upper[0]), owner(lower[0]))
        row = jnp.where(top, row + upper[1] * 128, row - 128 + lower[1] * 128)
        slot = (row // 16) * 128 + core * 64 + at * 16 + row % 16
        picks[...] = jnp.where(slots[...] == slot, 1.0, 0.0).astype(jnp.bfloat16)

        def piece(begin, size):
            value = jnp.dot(picks[...], everyone[:, pl.ds(begin, size)], preferred_element_type=jnp.float32)
            raw[:, pl.ds(begin, size)] = value.astype(jnp.bfloat16)

        @pl.loop(0, 8)
        def _(n):
            piece(pl.multiple_of(n * 256, 256), 256)

        piece(2048, 128)
        square = raw[:, 2048:2049].astype(jnp.float32) + raw[:, 2049:2050].astype(jnp.float32)
        inverse = lax.rsqrt(square / D + 1e-06)
        rows[...] = (raw[:, :2048].astype(jnp.float32) * inverse * gain[...]).astype(jnp.bfloat16)
        for base, (step, half) in zip((0, 128), (upper, lower)):
            found = raw[pl.ds(pl.multiple_of(base + lax.rem(me, 8) * 16, 16), 16), :2048]
            here = me // 8 == half
            strip[step] = jnp.where(here, found, strip[step])

    def multiply(step, group, first=False):
        def piece(begin, size):
            for half in range(2):
                value = lax.dot_general(
                    rows[...], weights[half, pl.ds(begin, size), :], (((1,), (1,)), ((), ())),
                    preferred_element_type=jnp.float32,
                )
                parts[step, half, :, pl.ds(begin, size)] = value.astype(jnp.bfloat16)

        if first:
            for n in range(4 * group, 4 * group + 4):
                for copy in weight_copies(n):
                    copy.wait()
        full = 4 if group == 0 else 3

        @pl.loop(0, full)
        def _(n):
            piece(pl.multiple_of(GROUPS[group][0] + n * 256, 256), 256)

        if group == 1:
            piece(1792, 128)

    def cut(ref, sub):
        begin, size = GROUPS[sub % 2]
        return ref.at[:, pl.ds(sub // 2 * 128, 128), pl.ds(begin, size)]

    sent = []

    def part_slot(kind, index):
        return came.at[kind * 2 + index, :, :, pl.ds(0, GROUPS[index][1])]

    part_sends = {}

    def pass_part(kind, index, src, way, step):
        at = kind * 2 + index
        copy = remote(src, part_slot(kind, index), psend.at[at], precv.at[at], along_x(way))
        copy.start()
        part_sends.setdefault(step, []).append(copy)

    def part_landed(kind, index):
        at = kind * 2 + index
        landing = part_slot(kind, index)
        remote(landing, landing, psend.at[at], precv.at[at], along_x(1)).wait_recv()
        return landing

    pick(2)
    for index in range(2):
        multiply(2, index, True)
        if index == 0:
            greet(plane_neighbours() + [along_x(step) for step in (1, 3)] + [partner()])
        pass_part(0, index, cut(parts.at[2], index), 1, 2)
        pass_part(3, index, cut(parts.at[2], 2 + index), 3, 2)
    pick(1)
    for index in range(2):
        multiply(1, index)
        pass_part(1, index, cut(parts.at[1], index), 1, 1)
        pass_part(4, index, cut(parts.at[1], 2 + index), 3, 1)
    pick(3)
    for index in range(2):
        multiply(3, index)
        for kind, sub, way in ((0, index, 1), (3, 2 + index, 3)):
            arrived = part_landed(kind, index)
            target = cut(parts.at[3], sub)
            target[...] = (target[...].astype(jnp.float32) + arrived[...].astype(jnp.float32)).astype(jnp.bfloat16)
            pass_part(kind + 2, index, target, way, 3)
    pick(0)
    for index in range(2):
        multiply(0, index)

    def hidden_piece(step, sub):
        begin, size = GROUPS[sub % 2]
        return hidden.at[owner(step), pl.ds(sub // 2 * 128, 128), pl.ds(begin, size)]

    def pass_hidden(at, piece, step):
        copy = remote(piece, piece, hsend.at[at], hrecv.at[at], along_x(step))
        copy.start()
        sent.append(copy)

    def hidden_landed(at, piece):
        remote(piece, piece, hsend.at[at], hrecv.at[at], along_x(1)).wait_recv()

    for index in range(2):
        for sub, near, far in ((index, 4, 2), (2 + index, 1, 5)):
            one = part_landed(near, index)
            two = part_landed(far, index)
            own = cut(parts.at[0], sub)
            gate, up = [
                own[half].astype(jnp.float32) + one[half].astype(jnp.float32) + two[half].astype(jnp.float32)
                for half in range(2)
            ]
            piece = hidden_piece(0, sub)
            piece[...] = (gate / (1.0 + jnp.exp(-gate)) * up).astype(jnp.bfloat16)
            pass_hidden(sub, piece, 1)
            pass_hidden(4 + sub, piece, 3)
    for copy in down_copies():
        copy.wait()

    def project(step):
        at = owner(step)
        for copy in part_sends.get(step, []):
            copy.wait_send()
        for side in range(2):
            @pl.loop(0, 4)
            def _(n):
                begin = pl.multiple_of(n * 256, 256)
                value = jnp.dot(
                    hidden[at],
                    downs[:, pl.ds(pl.multiple_of(side * 1024 + begin, 256), 256)],
                    preferred_element_type=jnp.float32,
                )
                parts[step, side, :, pl.ds(begin, 256)] = value.astype(jnp.bfloat16)

    def reduction(step):
        def term(t, at):
            return parts.at[step, at // 2, pl.ds(pl.multiple_of(t * 16, 16), 16), pl.ds(at % 2 * 512, 512)]

        def emit(at, value):
            total = value + strip[step, :, pl.ds(at * 512, 512)].astype(jnp.float32)
            target = pl.ds(pl.multiple_of(owner(step) * 16, 16), 16)
            fin[at // 2, target, pl.ds(at % 2 * 512, 512)] = total.astype(jnp.bfloat16)

        return reduce_plane(
            term, got.at[step], made.at[step], sums.at[step], send.at[step], recv.at[step], emit, False
        )

    def relay(index):
        hidden_landed(index, hidden_piece(3, index))
        pass_hidden(8 + index, hidden_piece(3, index), 1)
        hidden_landed(4 + 2 + index, hidden_piece(1, 2 + index))
        pass_hidden(10 + index, hidden_piece(1, 2 + index), 3)

    flows = {step: reduction(step) for step in range(4)}
    project(0)
    next(flows[0])
    relay(0)
    next(flows[0])
    relay(1)
    next(flows[0])
    for index in range(2):
        hidden_landed(2 + index, hidden_piece(3, 2 + index))
    project(3)
    next(flows[3])
    for index in range(2):
        hidden_landed(4 + index, hidden_piece(1, index))
    project(1)
    next(flows[1])
    next(flows[0])
    next(flows[3])
    next(flows[1])
    for index in range(2):
        hidden_landed(8 + index, hidden_piece(2, index))
        hidden_landed(10 + index, hidden_piece(2, 2 + index))
    project(2)
    next(flows[2])
    next(flows[3])
    next(flows[1])
    next(flows[2])
    next(flows[3])
    next(flows[1])
    next(flows[2])
    run(flows[0])
    run(flows[3])
    run(flows[1])
    run(flows[2])
    mine = pl.ds(pl.multiple_of(core * 64, 64), 64)
    theirs = pl.ds(pl.multiple_of((1 - core) * 64, 64), 64)
    swap = remote(fin.at[1 - core], out.at[mine, :], fsend, frecv, partner())
    swap.start()
    out[mine, :] = fin[core]
    swap.wait_send()
    landing = out.at[theirs, :]
    remote(landing, landing, fsend, frecv, partner()).wait_recv()
    for copy in sent + part_sends.get(0, []):
        copy.wait_send()


def feed_forward(everyone, slots, gain, w_own, w_other, d_own, d_other, collective_id):
    anywhere = pl.BlockSpec(memory_space=pl.ANY)
    vmem = pl.BlockSpec(memory_space=pltpu.VMEM)
    dma = pltpu.SemaphoreType.DMA
    bf16 = jnp.bfloat16
    return pl.pallas_call(
        feed_forward_kernel,
        out_shape=jax.ShapeDtypeStruct((128, 1024), bf16),
        in_specs=[vmem, vmem, vmem, anywhere, anywhere, anywhere, anywhere],
        out_specs=vmem,
        scratch_shapes=[
            pltpu.VMEM((2, PADDED, 2048), bf16),
            pltpu.VMEM((PADDED, 2048), bf16),
            pltpu.VMEM((256, 2048), bf16),
            pltpu.VMEM((256, WIDE), bf16),
            pltpu.VMEM((256, 2048), bf16),
            pltpu.VMEM((4, 16, 2048), bf16),
            pltpu.VMEM((4, 2, 256, PADDED), bf16),
            pltpu.VMEM((12, 2, 128, 1024), bf16),
            pltpu.VMEM((4, 256, PADDED), bf16),
            pltpu.VMEM((4, 60, 16, 512), bf16),
            pltpu.VMEM((4, 20, 16, 512), bf16),
            pltpu.VMEM((4, 16, 16, 512), bf16),
            pltpu.VMEM((2, 64, 1024), bf16),
            dma((8, 2)),
            dma((2,)),
            dma((12,)),
            dma((12,)),
            dma((12,)),
            dma((12,)),
            dma((4, 60)),
            dma((4, 60)),
            dma,
            dma,
        ],
        compiler_params=pltpu.CompilerParams(
            collective_id=collective_id, has_side_effects=True, vmem_limit_bytes=67043328
        ),
        name="feed_forward",
    )(everyone, slots, gain, w_own, w_other, d_own, d_other)


def local(
    vit_input,
    image_lengths,
    positions,
    vit_ln_gain,
    w_qkv,
    w_proj,
    merger_ln_gain,
    merger_w1,
    merger_w2,
    norm_gain,
    gate_up_weight,
    down_weight,
):
    seq_size = lax.axis_size("seq")
    core = lax.rem(lax.axis_index("seq"), 2)
    swap = [(i, i ^ 1) for i in range(seq_size)]
    gate_up_rows = jnp.transpose(gate_up_weight, (1, 2, 0))
    other_rows = lax.ppermute(gate_up_rows, "seq", swap)
    other_down = lax.ppermute(down_weight, "seq", swap)
    other_gain = lax.ppermute(norm_gain, "seq", swap)
    everyone = vision(
        vit_input,
        jnp.broadcast_to(image_lengths[0, 0] * 4, (8, 128)),
        vit_ln_gain[None],
        merger_ln_gain[None],
        jnp.transpose(w_qkv, (1, 2, 0)),
        w_proj,
        jnp.transpose(merger_w1),
        merger_w2,
        1,
    ).reshape(-1, WIDE)
    slots = positions.reshape(4, 2, 16, 16).transpose(1, 2, 0, 3).reshape(1, -1)
    gain = jnp.where(
        core == 0, jnp.concatenate([norm_gain, other_gain]), jnp.concatenate([other_gain, norm_gain])
    )
    return feed_forward(
        everyone, slots, gain[None], gate_up_rows, other_rows, down_weight, other_down, 2
    )


def solution(mesh):
    finer = Mesh(mesh.devices.reshape(mesh.shape["seq"], 4, 4), ("seq", "tp_0", "tp_1"))
    in_specs = (
        P(SEQ_TP, None),
        P("seq", None),
        P(),
        P(),
        P(None, None, TP),
        P(TP, None),
        P(),
        P(None, TP),
        P(TP, None),
        P("seq"),
        P("seq", None, TP),
        P(TP, "seq"),
    )
    out_specs = P(TP, "seq")
    return jax.shard_map(local, mesh=finer, in_specs=in_specs, out_specs=out_specs, check_vma=False)
```

profile of v0, /device:TPU:1, one launch (start us, length us, event | category | flops | bytes accessed | tf_op | source)
XLA Modules:
  0.0 286.2 jit_solution(2708668034368604997)
XLA Ops:
  0.0 1.4 collective-permute-start.1
  1.4 0.0 collective-permute-start.2
  1.4 0.5 collective-permute-start
  1.9 1.3 broadcast_in_dim.11.ln_gain
  3.2 1.3 broadcast_in_dim.12.merger_gain
  4.5 0.8 reshape.67
  5.3 0.7 reshape.68.slots
  6.7 0.6 broadcast_in_dim.10.ends
  7.3 0.0 copy-start
  7.3 137.8 %vision.1 = bf16[2,16,64,2176]{3,2,1,0:T(8,128)(2,1)} custom-call(bf16[64,1280]{1,0:T(8,128)(2,1)} %vit.1, s32[8,128]{1,0:T(8,128)} %broadcast_in_dim.10.ends, f32[1,1280]{1,0:T(1,128)} %broadcast_in_dim.11.ln_gain, f32[1,1280]{1,0:T(1,128)} %broadcast_in_dim.12.merger_gain, bf16[3,80,1280]{2,1,0:T(8,128)(2,1)} %bitcast.13, bf16[80,1280]{1,0:T(8,128)(2,1)} %w_proj.1, ...), custom_call_target="tpu_custom_call" | custom-call | tf_op jit(solution)/shard_map/vision/pallas_call | solution.py:494
  145.0 0.0 collective-permute-done
  145.0 0.0 copy-done
  145.1 0.6 broadcast_select_fusion.gain
  145.7 0.0 collective-permute-done.2.d_other
  145.7 0.0 collective-permute-done.1.w_other
  145.7 138.9 %feed_forward.1 = bf16[128,1024]{1,0:T(8,128)(2,1)} custom-call(bf16[2048,2176]{1,0:T(8,128)(2,1)} %bitcast.9, s32[1,2048]{1,0:T(1,128)} %reshape.68.slots, f32[1,2048]{1,0:T(1,128)} %broadcast_select_fusion.gain, bf16[2,1848,1024]{2,1,0:T(8,128)(2,1)} %bitcast.11, bf16[2,1848,1024]{2,1,0:T(8,128)(2,1)} %collective-permute-done.1.w_other, ...), custom_call_target="tpu_custom_call" | custom-call | tf_op jit(solution)/shard_map/feed_forward/pallas_call | solution.py:791
  284.5 1.7 copy.15
  (1 shorter events, 0.0 us)
Async XLA Ops:
  0.0 145.7 %collective-permute-start.1 = (bf16[2,1848,1024]{2,1,0:T(8,128)(2,1)}, bf16[2,1848,1024]{2,1,0:T(8,128)(2,1)}, u32[]{:S(2)}, u32[]{:S(2)}) collective-permute-start(bf16[2,1848,1024]{2,1,0:T(8,128)(2,1)} %bitcast.10), channel_id=1, source_target_pairs={{0,16},{16,0},{32,48},{48,32},{64,80},{80,64},{96,112},{112,96},{1... | collective-permute-start | bytes 22708232 | tf_op jit(solution)/shard_map/ppermute | solution.py:846
  1.4 144.3 %collective-permute-start.2 = (bf16[1848,1024]{1,0:T(8,128)(2,1)}, bf16[1848,1024]{1,0:T(8,128)(2,1)}, u32[]{:S(2)}, u32[]{:S(2)}) collective-permute-start(bf16[1848,1024]{1,0:T(8,128)(2,1)} %d_own.1), channel_id=1, source_target_pairs={{0,16},{16,0},{32,48},{48,32},{64,80},{80,64},{96,112},{112,96},{1... | collective-permute-start | bytes 11354120 | tf_op jit(solution)/shard_map/ppermute | solution.py:847
  1.4 143.7 %collective-permute-start = (f32[1024]{0:T(1024)}, f32[1024]{0:T(1024)S(1)}, u32[]{:S(2)}, u32[]{:S(2)}) collective-permute-start(f32[1024]{0:T(1024)} %param.21), channel_id=1, source_target_pairs={{0,16},{16,0},{32,48},{48,32},{64,80},{80,64},{96,112},{112,96},{1... | collective-permute-start | bytes 12296 | tf_op jit(solution)/shard_map/ppermute | solution.py:848
  7.3 137.8 %copy-start = (f32[1024]{0:T(1024)S(1)}, f32[1024]{0:T(1024)}, u32[]{:S(2)}) copy-start(f32[1024]{0:T(1024)} %param.21) | copy-start | bytes 12292
where the time goes:
time: 286 us
  Pallas kernels  277 us (97%)
  local copies, waits for them, and re-layouts  6.38 us (2%)
    pallas_call x1, Pallas kernels, feed_forward(): pl.pallas_call(feed_forward_kernel, out_shape=jax.ShapeDtypeStruct((128,...  139 us
    pallas_call x1, Pallas kernels, vision(): pl.pallas_call(vision_kernel, out_shape=jax.ShapeDtypeStruct((2, 16, 64,...  138 us
  transfers between devices with their start and end apart: 3, of which 0 were waited for; matrix products, arithmetic and copies ran while one was open for 2% of the time, Pallas kernels for 48%

commit v1 on v0

--- a/solution.py
+++ b/solution.py
@@ -211,14 +211,9 @@
         return phase_source(half, 4)
 
     for half in both:
-        raw(half, order[0])
-    for half in both:
-        raw(half, order[1])
-    if not eager:
-        for phase in order[2:]:
-            for half in both:
-                raw(half, phase)
-    yield
+        for phase in order[:2] if eager else order:
+            raw(half, phase)
+        yield
     for at, phase in enumerate(order):
         for half in both:
             summed(half, phase)
@@ -291,8 +286,8 @@
 def vision_kernel(
     vit, ends, ln_gain, merger_gain, w_qkv, w_proj, w_one, w_two, out,
     own, patches, qkv, wq, wp, att, heads, lined, tiles, block_in, merged, one, expanded, two, terms,
-    got, made, sums, parcels, block,
-    wsem, asend, arecv, psend, precv, qsend, qrecv, hsend, hrecv, msend, mrecv,
+    got, made, sums, parcels, block, held,
+    wsem, osem, asend, arecv, psend, precv, qsend, qrecv, hsend, hrecv, msend, mrecv,
     send, recv, xsend, xrecv, gsend, grecv, dsend, drecv,
 ):
     seq = lax.axis_index("seq")
@@ -323,14 +318,14 @@
     barrier = pltpu.get_barrier_semaphore()
     for target in targets:
         pl.semaphore_signal(barrier, inc=1, device_id=target, device_id_type=MESH_ID)
-    own[...] = norm_rows(vit[...].astype(jnp.float32), ln_gain[...]).astype(jnp.bfloat16)
+    own[...] = norm_rows(vit[...].astype(jnp.float32), ln_gain[...][None]).astype(jnp.bfloat16)
     pl.semaphore_wait(barrier, len(targets))
 
     rows_half = lambda ref, half: ref.at[pl.ds(half * 32, 32), :]
     rows_quarter = lambda ref, at: ref.at[pl.ds(at * 16, 16), :]
     patches[me] = own[...]
-    run(gather_plane(own, lambda t: patches.at[t], rows_half, rows_quarter, asend, arecv))
-
+    arrive = gather_plane(own, lambda t: patches.at[t], rows_half, rows_quarter, asend, arecv)
+    next(arrive)
     loads[1].wait()
     shared, awaited = [], []
     weights = gather_plane(
@@ -343,6 +338,13 @@
         share_with_partner(proj_slot, core, qsend, qrecv, shared, awaited),
     )
     next(weights)
+    next(arrive)
+    next(arrive)
+    next(arrive)
+    next(weights)
+    next(arrive)
+    next(weights)
+    run(arrive)
     loads[0].wait()
 
     @pl.loop(0, 4)
@@ -355,7 +357,7 @@
             ).astype(jnp.bfloat16)
 
     next(weights)
-    end = ends[0:1, 0:1]
+    end = ends[0:1, 0:1] * 4
 
     def attend_rows(n):
         rows = pl.ds(pl.multiple_of(n * 256, 256), 256)
@@ -378,14 +380,14 @@
         def _(at):
             attend_rows(at)
 
-        next(weights)
+        if n == 0:
+            next(weights)
     sent = []
     for at, offset in enumerate(others):
         copy = remote(att.at[peer_index(*offset)], heads.at[me], hsend.at[at], hrecv.at[at], peer(*offset))
         copy.start()
         sent.append(copy)
     heads[me] = att[me]
-    next(weights)
     run(weights)
     for copy in shared:
         copy.wait_send()
@@ -402,7 +404,7 @@
     def _(head):
         lined[...] += jnp.dot(heads[head, :, :80], wp[head], preferred_element_type=jnp.float32)
 
-    ready = norm_rows(lined[...], merger_gain[...])
+    ready = norm_rows(lined[...], merger_gain[...][None])
     for tile in range(10):
         tiles[tile] = ready[:, tile * 128 : tile * 128 + 128]
     for at in range(4):
@@ -425,12 +427,13 @@
     expanded[...] = (0.5 * total * (1.0 + lax.erf(total * (0.5 ** 0.5)))).astype(jnp.bfloat16)
     loads[3].wait()
 
-    @pl.loop(0, 16)
-    def _(n):
-        columns = pl.ds(pl.multiple_of(n * 512, 512), 512)
-        terms[:, columns] = jnp.dot(
-            expanded[...], two[:, columns], preferred_element_type=jnp.float32
-        ).astype(jnp.bfloat16)
+    def share_of(half):
+        @pl.loop(8 * half, 8 * half + 8)
+        def _(n):
+            columns = pl.ds(pl.multiple_of(n * 512, 512), 512)
+            terms[:, columns] = jnp.dot(
+                expanded[...], two[:, columns], preferred_element_type=jnp.float32
+            ).astype(jnp.bfloat16)
 
     def emit(at, value):
         parcels[at, :, :2048] = value.astype(jnp.bfloat16)
@@ -438,7 +441,11 @@
     def term(t, at):
         return terms.at[pl.ds(pl.multiple_of(t * 16, 16), 16), pl.ds(at * 2048, 2048)]
 
-    run(reduce_plane(term, got, made, sums, send, recv, emit))
+    shares = reduce_plane(term, got, made, sums, send, recv, emit)
+    share_of(0)
+    next(shares)
+    share_of(1)
+    run(shares)
     squares = jnp.zeros((16, 1), jnp.float32)
     for at in range(4):
         values = parcels[at, :, :2048].astype(jnp.float32)
@@ -449,41 +456,48 @@
     tail = jnp.where(lane == 0, high, jnp.where(lane == 1, low, 0.0)).astype(jnp.bfloat16)
     for at in range(4):
         parcels[at, :, 2048:] = tail
-    mine = pl.ds(pl.multiple_of(x * 16, 16), 16)
     sent = []
     for step in (2, 1, 3):
         copy = remote(
-            parcels.at[lax.rem(x + step, 4)], block.at[mine, :], xsend.at[step], xrecv.at[step], along_x(step)
+            parcels.at[lax.rem(x + step, 4)], block.at[x], xsend.at[step], xrecv.at[step], along_x(step)
         )
         copy.start()
         sent.append(copy)
-    block[mine, :] = parcels[x]
+    block[x] = parcels[x]
     for step in (1, 3, 2):
-        rows = pl.ds(pl.multiple_of(lax.rem(x + 4 - step, 4) * 16, 16), 16)
-        landing = block.at[rows, :]
+        landing = block.at[lax.rem(x + 4 - step, 4)]
         remote(landing, landing, xsend.at[step], xrecv.at[step], along_x(step)).wait_recv()
     for copy in sent:
         copy.wait_send()
     forwarded, expected = [], []
-    own_copy = remote(block, out.at[core, me], dsend.at[40], drecv.at[40], partner())
+
+    def spot(side, t):
+        return held.at[:, side, t]
+
+    own_copy = remote(block, spot(core, me), dsend.at[40], drecv.at[40], partner())
     own_copy.start()
-    out[core, me] = block[...]
+    held[:, core, me] = block[...]
     run(gather_plane(
         block,
-        lambda t: out.at[core, t],
-        rows_half,
-        rows_quarter,
+        lambda t: spot(core, t),
+        lambda ref, half: ref.at[pl.ds(half * 2, 2)],
+        lambda ref, at: ref.at[pl.ds(at, 1)],
         gsend,
         grecv,
-        share_with_partner(lambda side, t: out.at[side, t], core, dsend, drecv, forwarded, expected),
+        share_with_partner(spot, core, dsend, drecv, forwarded, expected),
     ))
-    other = out.at[1 - core, me]
+    copies = [pltpu.make_async_copy(held.at[:, side], out.at[:, side], osem.at[at]) for at, side in enumerate((core, 1 - core))]
+    copies[0].start()
+    other = spot(1 - core, me)
     expected.append(remote(other, other, dsend.at[40], drecv.at[40], partner()))
+    for copy in expected:
+        copy.wait_recv()
+    copies[1].start()
     own_copy.wait_send()
     for copy in forwarded:
         copy.wait_send()
-    for copy in expected:
-        copy.wait_recv()
+    for copy in copies:
+        copy.wait()
 
 
 def vision(vit, ends, ln_gain, merger_gain, w_qkv, w_proj, w_one, w_two, collective_id):
@@ -493,9 +507,9 @@
     bf16 = jnp.bfloat16
     return pl.pallas_call(
         vision_kernel,
-        out_shape=jax.ShapeDtypeStruct((2, 16, 64, WIDE), bf16),
+        out_shape=jax.ShapeDtypeStruct((4, 2, 16, 16, WIDE), bf16),
         in_specs=[vmem] * 4 + [anywhere] * 4,
-        out_specs=vmem,
+        out_specs=anywhere,
         scratch_shapes=[
             pltpu.VMEM((64, 1280), bf16),
             pltpu.VMEM((16, 64, 1280), bf16),
@@ -516,8 +530,10 @@
             pltpu.VMEM((20, 16, 2048), bf16),
             pltpu.VMEM((16, 16, 2048), bf16),
             pltpu.VMEM((4, 16, WIDE), bf16),
-            pltpu.VMEM((64, WIDE), bf16),
+            pltpu.VMEM((4, 16, WIDE), bf16),
+            pltpu.VMEM((4, 2, 16, 16, WIDE), bf16),
             dma((4,)),
+            dma((2,)),
             dma((40,)), dma((40,)),
             dma((40,)), dma((40,)),
             dma((40,)), dma((40,)),
@@ -535,19 +551,29 @@
     )(vit, ends, ln_gain, merger_gain, w_qkv, w_proj, w_one, w_two)
 
 
-GROUPS = ((0, 1024), (1024, 896))
+GROUPS = ((0, 512), (512, 1408))
 BLOCKS = (((0, 0), (0, 1)), ((1, 1), (3, 0)), ((2, 0), (2, 1)), ((1, 0), (3, 1)))
 
 
 def feed_forward_kernel(
-    everyone, slots, gain, w_own, w_other, d_own, d_other, out,
-    weights, downs, picks, raw, rows, strip, parts, came, hidden, got, made, sums, fin,
-    wsem, osem, psend, precv, hsend, hrecv, send, recv, fsend, frecv,
+    tokens, slots, own_gain, other_gain, w_own, w_other, d_own, d_other, out,
+    weights, downs, everyone, gain, picks, raw, rows, strip, parts, came_first, came_second, hidden, got, made, sums, fin,
+    esem, wsem, osem, psend, precv, hsend, hrecv, send, recv, fsend, frecv,
 ):
     seq = lax.axis_index("seq")
     x, core = seq // 2, lax.rem(seq, 2)
     me = lax.axis_index("tp_0") * 4 + lax.axis_index("tp_1")
     real = w_own.shape[1]
+    wide = [(n * 256, 256 if n < 8 else 128) for n in range(9)]
+    entering = [
+        pltpu.make_async_copy(tokens.at[:, pl.ds(*cut)], everyone.at[:, pl.ds(*cut)], esem.at[n])
+        for n, cut in enumerate(wide)
+    ]
+    for copy in entering:
+        copy.start()
+    first_core = core == 0
+    gain[:, :1024] = jnp.where(first_core, own_gain[...], other_gain[...])[None]
+    gain[:, 1024:] = jnp.where(first_core, other_gain[...], own_gain[...])[None]
     weights[:, pl.ds(1840, 80), :] = jnp.zeros((2, 80, 2048), jnp.bfloat16)
     downs[pl.ds(1840, 80), :] = jnp.zeros((80, 2048), jnp.bfloat16)
     sides = ((w_own, d_own, core), (w_other, d_other, 1 - core))
@@ -581,24 +607,29 @@
     def owner(step):
         return lax.rem(x + step, 4)
 
-    def pick(block):
+    def pick(block, first=False):
         upper, lower = BLOCKS[block]
         row = lax.broadcasted_iota(jnp.int32, (256, 1), 0)
         top = row < 128
         at = jnp.where(top, owner(upper[0]), owner(lower[0]))
         row = jnp.where(top, row + upper[1] * 128, row - 128 + lower[1] * 128)
         slot = (row // 16) * 128 + core * 64 + at * 16 + row % 16
-        picks[...] = jnp.where(slots[...] == slot, 1.0, 0.0).astype(jnp.bfloat16)
+        picks[...] = jnp.where(slots[...][None] == slot, 1.0, 0.0).astype(jnp.bfloat16)
 
         def piece(begin, size):
             value = jnp.dot(picks[...], everyone[:, pl.ds(begin, size)], preferred_element_type=jnp.float32)
             raw[:, pl.ds(begin, size)] = value.astype(jnp.bfloat16)
 
-        @pl.loop(0, 8)
-        def _(n):
-            piece(pl.multiple_of(n * 256, 256), 256)
-
-        piece(2048, 128)
+        if first:
+            for n, cut in enumerate(wide):
+                entering[n].wait()
+                piece(*cut)
+        else:
+            @pl.loop(0, 8)
+            def _(n):
+                piece(pl.multiple_of(n * 256, 256), 256)
+
+            piece(2048, 128)
         square = raw[:, 2048:2049].astype(jnp.float32) + raw[:, 2049:2050].astype(jnp.float32)
         inverse = lax.rsqrt(square / D + 1e-06)
         rows[...] = (raw[:, :2048].astype(jnp.float32) * inverse * gain[...]).astype(jnp.bfloat16)
@@ -617,10 +648,10 @@
                 parts[step, half, :, pl.ds(begin, size)] = value.astype(jnp.bfloat16)
 
         if first:
-            for n in range(4 * group, 4 * group + 4):
+            for n in (range(2), range(2, 8))[group]:
                 for copy in weight_copies(n):
                     copy.wait()
-        full = 4 if group == 0 else 3
+        full = 2 if group == 0 else 5
 
         @pl.loop(0, full)
         def _(n):
@@ -636,7 +667,7 @@
     sent = []
 
     def part_slot(kind, index):
-        return came.at[kind * 2 + index, :, :, pl.ds(0, GROUPS[index][1])]
+        return (came_first, came_second)[index].at[kind]
 
     part_sends = {}
 
@@ -652,7 +683,7 @@
         remote(landing, landing, psend.at[at], precv.at[at], along_x(1)).wait_recv()
         return landing
 
-    pick(2)
+    pick(2, True)
     for index in range(2):
         multiply(2, index, True)
         if index == 0:
@@ -709,6 +740,9 @@
         for copy in part_sends.get(step, []):
             copy.wait_send()
         for side in range(2):
+            if side == 1:
+                next(flows[step])
+
             @pl.loop(0, 4)
             def _(n):
                 begin = pl.multiple_of(n * 256, 256)
@@ -719,6 +753,8 @@
                 )
                 parts[step, side, :, pl.ds(begin, 256)] = value.astype(jnp.bfloat16)
 
+        next(flows[step])
+
     def reduction(step):
         def term(t, at):
             return parts.at[step, at // 2, pl.ds(pl.multiple_of(t * 16, 16), 16), pl.ds(at % 2 * 512, 512)]
@@ -740,7 +776,6 @@
 
     flows = {step: reduction(step) for step in range(4)}
     project(0)
-    next(flows[0])
     relay(0)
     next(flows[0])
     relay(1)
@@ -748,11 +783,9 @@
     for index in range(2):
         hidden_landed(2 + index, hidden_piece(3, 2 + index))
     project(3)
-    next(flows[3])
     for index in range(2):
         hidden_landed(4 + index, hidden_piece(1, index))
     project(1)
-    next(flows[1])
     next(flows[0])
     next(flows[3])
     next(flows[1])
@@ -760,7 +793,6 @@
         hidden_landed(8 + index, hidden_piece(2, index))
         hidden_landed(10 + index, hidden_piece(2, 2 + index))
     project(2)
-    next(flows[2])
     next(flows[3])
     next(flows[1])
     next(flows[2])
@@ -783,7 +815,7 @@
         copy.wait_send()
 
 
-def feed_forward(everyone, slots, gain, w_own, w_other, d_own, d_other, collective_id):
+def feed_forward(everyone, slots, own_gain, other_gain, w_own, w_other, d_own, d_other, collective_id):
     anywhere = pl.BlockSpec(memory_space=pl.ANY)
     vmem = pl.BlockSpec(memory_space=pltpu.VMEM)
     dma = pltpu.SemaphoreType.DMA
@@ -791,22 +823,26 @@
     return pl.pallas_call(
         feed_forward_kernel,
         out_shape=jax.ShapeDtypeStruct((128, 1024), bf16),
-        in_specs=[vmem, vmem, vmem, anywhere, anywhere, anywhere, anywhere],
+        in_specs=[anywhere, vmem, vmem, vmem, anywhere, anywhere, anywhere, anywhere],
         out_specs=vmem,
         scratch_shapes=[
             pltpu.VMEM((2, PADDED, 2048), bf16),
             pltpu.VMEM((PADDED, 2048), bf16),
+            pltpu.VMEM((2048, WIDE), bf16),
+            pltpu.VMEM((1, 2048), jnp.float32),
             pltpu.VMEM((256, 2048), bf16),
             pltpu.VMEM((256, WIDE), bf16),
             pltpu.VMEM((256, 2048), bf16),
             pltpu.VMEM((4, 16, 2048), bf16),
             pltpu.VMEM((4, 2, 256, PADDED), bf16),
-            pltpu.VMEM((12, 2, 128, 1024), bf16),
+            pltpu.VMEM((6, 2, 128, 512), bf16),
+            pltpu.VMEM((6, 2, 128, 1408), bf16),
             pltpu.VMEM((4, 256, PADDED), bf16),
             pltpu.VMEM((4, 60, 16, 512), bf16),
             pltpu.VMEM((4, 20, 16, 512), bf16),
             pltpu.VMEM((4, 16, 16, 512), bf16),
             pltpu.VMEM((2, 64, 1024), bf16),
+            dma((9,)),
             dma((8, 2)),
             dma((2,)),
             dma((12,)),
@@ -822,7 +858,7 @@
             collective_id=collective_id, has_side_effects=True, vmem_limit_bytes=67043328
         ),
         name="feed_forward",
-    )(everyone, slots, gain, w_own, w_other, d_own, d_other)
+    )(everyone, slots, own_gain, other_gain, w_own, w_other, d_own, d_other)
 
 
 def local(
@@ -840,7 +876,6 @@
     down_weight,
 ):
     seq_size = lax.axis_size("seq")
-    core = lax.rem(lax.axis_index("seq"), 2)
     swap = [(i, i ^ 1) for i in range(seq_size)]
     gate_up_rows = jnp.transpose(gate_up_weight, (1, 2, 0))
     other_rows = lax.ppermute(gate_up_rows, "seq", swap)
@@ -848,21 +883,17 @@
     other_gain = lax.ppermute(norm_gain, "seq", swap)
     everyone = vision(
         vit_input,
-        jnp.broadcast_to(image_lengths[0, 0] * 4, (8, 128)),
-        vit_ln_gain[None],
-        merger_ln_gain[None],
+        image_lengths,
+        vit_ln_gain,
+        merger_ln_gain,
         jnp.transpose(w_qkv, (1, 2, 0)),
         w_proj,
         jnp.transpose(merger_w1),
         merger_w2,
         1,
     ).reshape(-1, WIDE)
-    slots = positions.reshape(4, 2, 16, 16).transpose(1, 2, 0, 3).reshape(1, -1)
-    gain = jnp.where(
-        core == 0, jnp.concatenate([norm_gain, other_gain]), jnp.concatenate([other_gain, norm_gain])
-    )
     return feed_forward(
-        everyone, slots, gain[None], gate_up_rows, other_rows, down_weight, other_down, 2
+        everyone, positions, norm_gain, other_gain, gate_up_rows, other_rows, down_weight, other_down, 2
     )
 
 

time: 286 us -> 270 us (0.944)
  Pallas kernels: 277 us -> 266 us
  local copies, waits for them, and re-layouts: 6.38 us -> 1.67 us
    pallas_call x1, Pallas kernels: 138 us -> 130 us  [vision(): pl.pallas_call(vision_kernel, out_shape=jax.ShapeDtypeStruct((4, 2, 16, 1...]
    broadcast_in_dim x3 -> x0, local copies, waits for them, and re-layouts: 3.18 us -> none  [the longest x1 1.29 us: local(): vit_ln_gain[None]]
    pallas_call x1, Pallas kernels: 139 us -> 136 us  [feed_forward(): pl.pallas_call(feed_forward_kernel, out_shape=jax.ShapeDtypeStruct((128,...]
  transfers between devices with their start and end apart: 3 -> 3, of which waited for: 0 -> 0; matrix products, arithmetic and copies ran while one was open for 2% -> 0% of each run, Pallas kernels for 48% -> 48%
where the time goes in v1:
time: 270 us
  Pallas kernels  266 us (99%)
    pallas_call x1, Pallas kernels, feed_forward(): pl.pallas_call(feed_forward_kernel, out_shape=jax.ShapeDtypeStruct((128,...  136 us
    pallas_call x1, Pallas kernels, vision(): pl.pallas_call(vision_kernel, out_shape=jax.ShapeDtypeStruct((4, 2, 16, 1...  130 us
  transfers between devices with their start and end apart: 3, of which 0 were waited for; matrix products, arithmetic and copies ran while one was open for 0% of the time, Pallas kernels for 48%

profile of v1, /device:TPU:1, one launch (start us, length us, event | category | flops | bytes accessed | tf_op | source)
XLA Modules:
  0.0 269.7 jit_solution(4364217831344546737)
XLA Ops:
  0.0 1.4 collective-permute-start.1
  1.4 0.0 collective-permute-start.2
  1.4 0.5 collective-permute-start
  1.9 130.2 %vision.1 = bf16[4,2,16,16,2176]{4,3,2,1,0:T(8,128)(2,1)} custom-call(bf16[64,1280]{1,0:T(8,128)(2,1)} %vit.1, s32[1,2]{1,0:T(1,128)} %ends.1, f32[1280]{0:T(1024)} %ln_gain.1, f32[1280]{0:T(1024)} %merger_gain.1, bf16[3,80,1280]{2,1,0:T(8,128)(2,1)} %bitcast.8, bf16[80,1280]{1,0:T(8,128)(2,1)} %w_proj.1, bf16[320,5120]{1,0:T(8,128)(2,1)} %bitcast.7, ...), custom_call_target="tpu_custom_call" | custom-call | tf_op jit(solution)/shard_map/vision/pallas_call | solution.py:508
  132.1 0.0 collective-permute-done.other_gain
  132.1 0.0 collective-permute-done.2.d_other
  132.2 0.0 collective-permute-done.1.w_other
  132.2 135.9 %feed_forward.1 = bf16[128,1024]{1,0:T(8,128)(2,1)} custom-call(bf16[2048,2176]{1,0:T(8,128)(2,1)} %bitcast.4, s32[2048]{0:T(1024)} %slots.1, f32[1024]{0:T(1024)} %own_gain.1, f32[1024]{0:T(1024)} %collective-permute-done.other_gain, bf16[2,1848,1024]{2,1,0:T(8,128)(2,1)} %bitcast.6, bf16[2,1848,1024]{2,1,0:T(8,128)(2,1)} %collective-permute-done.1.w_other, ...), custom_call_target="tpu_custom_call" | custom-call | tf_op jit(solution)/shard_map/feed_forward/pallas_call | solution.py:823
  268.1 1.7 copy.14
Async XLA Ops:
  0.0 132.2 %collective-permute-start.1 = (bf16[2,1848,1024]{2,1,0:T(8,128)(2,1)}, bf16[2,1848,1024]{2,1,0:T(8,128)(2,1)}, u32[]{:S(2)}, u32[]{:S(2)}) collective-permute-start(bf16[2,1848,1024]{2,1,0:T(8,128)(2,1)} %bitcast.5), channel_id=1, source_target_pairs={{0,16},{16,0},{32,48},{48,32},{64,80},{80,64},{96,112},{112,96},{1... | collective-permute-start | bytes 22708232 | tf_op jit(solution)/shard_map/ppermute | solution.py:881
  1.4 130.8 %collective-permute-start.2 = (bf16[1848,1024]{1,0:T(8,128)(2,1)}, bf16[1848,1024]{1,0:T(8,128)(2,1)}, u32[]{:S(2)}, u32[]{:S(2)}) collective-permute-start(bf16[1848,1024]{1,0:T(8,128)(2,1)} %d_own.1), channel_id=1, source_target_pairs={{0,16},{16,0},{32,48},{48,32},{64,80},{80,64},{96,112},{112,96},{1... | collective-permute-start | bytes 11354120 | tf_op jit(solution)/shard_map/ppermute | solution.py:882
  1.4 130.8 %collective-permute-start = (f32[1024]{0:T(1024)}, f32[1024]{0:T(1024)}, u32[]{:S(2)}, u32[]{:S(2)}) collective-permute-start(f32[1024]{0:T(1024)} %own_gain.1), channel_id=1, source_target_pairs={{0,16},{16,0},{32,48},{48,32},{64,80},{80,64},{96,112},{112,96},{1... | collective-permute-start | bytes 12296 | tf_op jit(solution)/shard_map/ppermute | solution.py:883

commit v2 on v1

--- a/solution.py
+++ b/solution.py
@@ -286,9 +286,9 @@
 def vision_kernel(
     vit, ends, ln_gain, merger_gain, w_qkv, w_proj, w_one, w_two, out,
     own, patches, qkv, wq, wp, att, heads, lined, tiles, block_in, merged, one, expanded, two, terms,
-    got, made, sums, parcels, block, held,
-    wsem, osem, asend, arecv, psend, precv, qsend, qrecv, hsend, hrecv, msend, mrecv,
-    send, recv, xsend, xrecv, gsend, grecv, dsend, drecv,
+    got, made, sums, parcels,
+    wsem, asend, arecv, psend, precv, qsend, qrecv, hsend, hrecv, msend, mrecv,
+    send, recv, xsend, xrecv,
 ):
     seq = lax.axis_index("seq")
     x, core = seq // 2, lax.rem(seq, 2)
@@ -312,7 +312,7 @@
         pltpu.make_async_copy(w_one, one, wsem.at[2]),
         pltpu.make_async_copy(w_two, two, wsem.at[3]),
     ]
-    for copy in loads:
+    for copy in loads[:2]:
         copy.start()
     targets = [peer(*offset) for offset in others] + [along_x(step) for step in (1, 2, 3)] + [partner()]
     barrier = pltpu.get_barrier_semaphore()
@@ -339,9 +339,11 @@
     )
     next(weights)
     next(arrive)
+    loads[2].start()
     next(arrive)
     next(arrive)
     next(weights)
+    loads[3].start()
     next(arrive)
     next(weights)
     run(arrive)
@@ -459,45 +461,16 @@
     sent = []
     for step in (2, 1, 3):
         copy = remote(
-            parcels.at[lax.rem(x + step, 4)], block.at[x], xsend.at[step], xrecv.at[step], along_x(step)
+            parcels.at[lax.rem(x + step, 4)], out.at[x], xsend.at[step], xrecv.at[step], along_x(step)
         )
         copy.start()
         sent.append(copy)
-    block[x] = parcels[x]
+    out[x] = parcels[x]
     for step in (1, 3, 2):
-        landing = block.at[lax.rem(x + 4 - step, 4)]
+        landing = out.at[lax.rem(x + 4 - step, 4)]
         remote(landing, landing, xsend.at[step], xrecv.at[step], along_x(step)).wait_recv()
     for copy in sent:
         copy.wait_send()
-    forwarded, expected = [], []
-
-    def spot(side, t):
-        return held.at[:, side, t]
-
-    own_copy = remote(block, spot(core, me), dsend.at[40], drecv.at[40], partner())
-    own_copy.start()
-    held[:, core, me] = block[...]
-    run(gather_plane(
-        block,
-        lambda t: spot(core, t),
-        lambda ref, half: ref.at[pl.ds(half * 2, 2)],
-        lambda ref, at: ref.at[pl.ds(at, 1)],
-        gsend,
-        grecv,
-        share_with_partner(spot, core, dsend, drecv, forwarded, expected),
-    ))
-    copies = [pltpu.make_async_copy(held.at[:, side], out.at[:, side], osem.at[at]) for at, side in enumerate((core, 1 - core))]
-    copies[0].start()
-    other = spot(1 - core, me)
-    expected.append(remote(other, other, dsend.at[40], drecv.at[40], partner()))
-    for copy in expected:
-        copy.wait_recv()
-    copies[1].start()
-    own_copy.wait_send()
-    for copy in forwarded:
-        copy.wait_send()
-    for copy in copies:
-        copy.wait()
 
 
 def vision(vit, ends, ln_gain, merger_gain, w_qkv, w_proj, w_one, w_two, collective_id):
@@ -507,9 +480,9 @@
     bf16 = jnp.bfloat16
     return pl.pallas_call(
         vision_kernel,
-        out_shape=jax.ShapeDtypeStruct((4, 2, 16, 16, WIDE), bf16),
+        out_shape=jax.ShapeDtypeStruct((4, 16, WIDE), bf16),
         in_specs=[vmem] * 4 + [anywhere] * 4,
-        out_specs=anywhere,
+        out_specs=vmem,
         scratch_shapes=[
             pltpu.VMEM((64, 1280), bf16),
             pltpu.VMEM((16, 64, 1280), bf16),
@@ -530,10 +503,7 @@
             pltpu.VMEM((20, 16, 2048), bf16),
             pltpu.VMEM((16, 16, 2048), bf16),
             pltpu.VMEM((4, 16, WIDE), bf16),
-            pltpu.VMEM((4, 16, WIDE), bf16),
-            pltpu.VMEM((4, 2, 16, 16, WIDE), bf16),
             dma((4,)),
-            dma((2,)),
             dma((40,)), dma((40,)),
             dma((40,)), dma((40,)),
             dma((40,)), dma((40,)),
@@ -541,8 +511,6 @@
             dma((40,)), dma((40,)),
             dma((60,)), dma((60,)),
             dma((4,)), dma((4,)),
-            dma((40,)), dma((40,)),
-            dma((41,)), dma((41,)),
         ],
         compiler_params=pltpu.CompilerParams(
             collective_id=collective_id, has_side_effects=True, vmem_limit_bytes=56 * 1024 * 1024
@@ -556,21 +524,14 @@
 
 
 def feed_forward_kernel(
-    tokens, slots, own_gain, other_gain, w_own, w_other, d_own, d_other, out,
-    weights, downs, everyone, gain, picks, raw, rows, strip, parts, came_first, came_second, hidden, got, made, sums, fin,
-    esem, wsem, osem, psend, precv, hsend, hrecv, send, recv, fsend, frecv,
+    block, slots, own_gain, other_gain, w_own, w_other, d_own, d_other, out,
+    weights, downs, everyone, gain, seats, picks, raw, rows, strip, parts, came_first, came_second, hidden, got, made, sums, fin,
+    gsend, grecv, dsend, drecv, wsem, osem, psend, precv, hsend, hrecv, send, recv, fsend, frecv,
 ):
     seq = lax.axis_index("seq")
     x, core = seq // 2, lax.rem(seq, 2)
     me = lax.axis_index("tp_0") * 4 + lax.axis_index("tp_1")
     real = w_own.shape[1]
-    wide = [(n * 256, 256 if n < 8 else 128) for n in range(9)]
-    entering = [
-        pltpu.make_async_copy(tokens.at[:, pl.ds(*cut)], everyone.at[:, pl.ds(*cut)], esem.at[n])
-        for n, cut in enumerate(wide)
-    ]
-    for copy in entering:
-        copy.start()
     first_core = core == 0
     gain[:, :1024] = jnp.where(first_core, own_gain[...], other_gain[...])[None]
     gain[:, 1024:] = jnp.where(first_core, other_gain[...], own_gain[...])[None]
@@ -597,39 +558,84 @@
             for side, (_, d, at) in enumerate(sides)
         ]
 
-    for n in range(8):
-        for copy in weight_copies(n):
-            copy.start()
-    for copy in down_copies():
-        copy.start()
     strip[...] = jnp.zeros_like(strip)
 
     def owner(step):
         return lax.rem(x + step, 4)
 
-    def pick(block, first=False):
-        upper, lower = BLOCKS[block]
+    greet(plane_neighbours() + [along_x(step) for step in (1, 3)] + [partner()])
+    forwarded, expected = [], []
+
+    def spot(side, t):
+        return everyone.at[:, side, t]
+
+    own_copy = remote(block, spot(core, me), dsend.at[40], drecv.at[40], partner())
+    own_copy.start()
+    everyone[:, core, me] = block[...]
+    arrive = gather_plane(
+        block,
+        lambda t: spot(core, t),
+        lambda ref, half: ref.at[pl.ds(half * 2, 2)],
+        lambda ref, at: ref.at[pl.ds(at, 1)],
+        gsend,
+        grecv,
+        share_with_partner(spot, core, dsend, drecv, forwarded, expected),
+    )
+    for turn in range(4):
+        next(arrive)
+        for n in (2 * turn, 2 * turn + 1):
+            for copy in weight_copies(n):
+                copy.start()
+    run(arrive)
+    other = spot(1 - core, me)
+    expected.append(remote(other, other, dsend.at[40], drecv.at[40], partner()))
+    seats_of_all = slots[...][None]
+    for side in range(2):
+        for at in range(4):
+            begin = at * 512 + side * 256
+            seats[side, :, pl.ds(at * 256, 256)] = seats_of_all[:, begin : begin + 256]
+
+    def pick(step, first=False):
+        upper, lower = BLOCKS[step]
         row = lax.broadcasted_iota(jnp.int32, (256, 1), 0)
         top = row < 128
         at = jnp.where(top, owner(upper[0]), owner(lower[0]))
         row = jnp.where(top, row + upper[1] * 128, row - 128 + lower[1] * 128)
         slot = (row // 16) * 128 + core * 64 + at * 16 + row % 16
-        picks[...] = jnp.where(slots[...][None] == slot, 1.0, 0.0).astype(jnp.bfloat16)
-
-        def piece(begin, size):
-            value = jnp.dot(picks[...], everyone[:, pl.ds(begin, size)], preferred_element_type=jnp.float32)
-            raw[:, pl.ds(begin, size)] = value.astype(jnp.bfloat16)
-
-        if first:
-            for n, cut in enumerate(wide):
-                entering[n].wait()
-                piece(*cut)
-        else:
+        for at, side in enumerate((core, 1 - core)):
+            picks[at] = jnp.where(seats[side] == slot, 1.0, 0.0).astype(jnp.bfloat16)
+
+        def found(at, columns):
+            side = core if at == 0 else 1 - core
+            some = everyone[:, side, :, :, columns].reshape(1024, columns.size)
+            return jnp.dot(picks[at], some, preferred_element_type=jnp.float32)
+
+        def over_columns(fill):
             @pl.loop(0, 8)
             def _(n):
-                piece(pl.multiple_of(n * 256, 256), 256)
-
-            piece(2048, 128)
+                fill(pl.ds(pl.multiple_of(n * 256, 256), 256))
+
+            fill(pl.ds(2048, 128))
+
+        def fill_own(columns):
+            raw[:, columns] = found(0, columns).astype(jnp.bfloat16)
+
+        def fill_other(columns):
+            raw[:, columns] = (raw[:, columns].astype(jnp.float32) + found(1, columns)).astype(jnp.bfloat16)
+
+        def fill_both(columns):
+            raw[:, columns] = (found(0, columns) + found(1, columns)).astype(jnp.bfloat16)
+
+        if first:
+            over_columns(fill_own)
+            for copy in expected:
+                copy.wait_recv()
+            own_copy.wait_send()
+            for copy in forwarded:
+                copy.wait_send()
+            over_columns(fill_other)
+        else:
+            over_columns(fill_both)
         square = raw[:, 2048:2049].astype(jnp.float32) + raw[:, 2049:2050].astype(jnp.float32)
         inverse = lax.rsqrt(square / D + 1e-06)
         rows[...] = (raw[:, :2048].astype(jnp.float32) * inverse * gain[...]).astype(jnp.bfloat16)
@@ -686,8 +692,6 @@
     pick(2, True)
     for index in range(2):
         multiply(2, index, True)
-        if index == 0:
-            greet(plane_neighbours() + [along_x(step) for step in (1, 3)] + [partner()])
         pass_part(0, index, cut(parts.at[2], index), 1, 2)
         pass_part(3, index, cut(parts.at[2], 2 + index), 3, 2)
     pick(1)
@@ -703,6 +707,8 @@
             target = cut(parts.at[3], sub)
             target[...] = (target[...].astype(jnp.float32) + arrived[...].astype(jnp.float32)).astype(jnp.bfloat16)
             pass_part(kind + 2, index, target, way, 3)
+    for copy in down_copies():
+        copy.start()
     pick(0)
     for index in range(2):
         multiply(0, index)
@@ -815,7 +821,7 @@
         copy.wait_send()
 
 
-def feed_forward(everyone, slots, own_gain, other_gain, w_own, w_other, d_own, d_other, collective_id):
+def feed_forward(block, slots, own_gain, other_gain, w_own, w_other, d_own, d_other, collective_id):
     anywhere = pl.BlockSpec(memory_space=pl.ANY)
     vmem = pl.BlockSpec(memory_space=pltpu.VMEM)
     dma = pltpu.SemaphoreType.DMA
@@ -823,14 +829,15 @@
     return pl.pallas_call(
         feed_forward_kernel,
         out_shape=jax.ShapeDtypeStruct((128, 1024), bf16),
-        in_specs=[anywhere, vmem, vmem, vmem, anywhere, anywhere, anywhere, anywhere],
+        in_specs=[vmem, vmem, vmem, vmem, anywhere, anywhere, anywhere, anywhere],
         out_specs=vmem,
         scratch_shapes=[
             pltpu.VMEM((2, PADDED, 2048), bf16),
             pltpu.VMEM((PADDED, 2048), bf16),
-            pltpu.VMEM((2048, WIDE), bf16),
+            pltpu.VMEM((4, 2, 16, 16, WIDE), bf16),
             pltpu.VMEM((1, 2048), jnp.float32),
-            pltpu.VMEM((256, 2048), bf16),
+            pltpu.VMEM((2, 1, 1024), jnp.int32),
+            pltpu.VMEM((2, 256, 1024), bf16),
             pltpu.VMEM((256, WIDE), bf16),
             pltpu.VMEM((256, 2048), bf16),
             pltpu.VMEM((4, 16, 2048), bf16),
@@ -842,7 +849,10 @@
             pltpu.VMEM((4, 20, 16, 512), bf16),
             pltpu.VMEM((4, 16, 16, 512), bf16),
             pltpu.VMEM((2, 64, 1024), bf16),
-            dma((9,)),
+            dma((40,)),
+            dma((40,)),
+            dma((41,)),
+            dma((41,)),
             dma((8, 2)),
             dma((2,)),
             dma((12,)),
@@ -858,7 +868,7 @@
             collective_id=collective_id, has_side_effects=True, vmem_limit_bytes=67043328
         ),
         name="feed_forward",
-    )(everyone, slots, own_gain, other_gain, w_own, w_other, d_own, d_other)
+    )(block, slots, own_gain, other_gain, w_own, w_other, d_own, d_other)
 
 
 def local(
@@ -881,7 +891,7 @@
     other_rows = lax.ppermute(gate_up_rows, "seq", swap)
     other_down = lax.ppermute(down_weight, "seq", swap)
     other_gain = lax.ppermute(norm_gain, "seq", swap)
-    everyone = vision(
+    block = vision(
         vit_input,
         image_lengths,
         vit_ln_gain,
@@ -891,9 +901,9 @@
         jnp.transpose(merger_w1),
         merger_w2,
         1,
-    ).reshape(-1, WIDE)
+    )
     return feed_forward(
-        everyone, positions, norm_gain, other_gain, gate_up_rows, other_rows, down_weight, other_down, 2
+        block, positions, norm_gain, other_gain, gate_up_rows, other_rows, down_weight, other_down, 2
     )
 
 

time: 270 us -> 269 us (level)
    pallas_call x1, Pallas kernels: 130 us -> 97 us  [vision(): pl.pallas_call(vision_kernel, out_shape=jax.ShapeDtypeStruct((4, 16, WIDE...]
    pallas_call x1, Pallas kernels: 136 us -> 168 us  [feed_forward(): pl.pallas_call(feed_forward_kernel, out_shape=jax.ShapeDtypeStruct((128,...]
  transfers between devices with their start and end apart: 3 -> 3, of which waited for: 0 -> 0; matrix products, arithmetic and copies ran while one was open for 0% -> 0% of each run, Pallas kernels for 48% -> 36%
where the time goes in v2:
time: 269 us; the launch traced here: 268 us
  Pallas kernels  265 us (99%)
    pallas_call x1, Pallas kernels, feed_forward(): pl.pallas_call(feed_forward_kernel, out_shape=jax.ShapeDtypeStruct((128,...  168 us
    pallas_call x1, Pallas kernels, vision(): pl.pallas_call(vision_kernel, out_shape=jax.ShapeDtypeStruct((4, 16, WIDE...  97 us
  transfers between devices with their start and end apart: 3, of which 0 were waited for; matrix products, arithmetic and copies ran while one was open for 0% of the time, Pallas kernels for 36%

profile of v2, /device:TPU:1, one launch (start us, length us, event | category | flops | bytes accessed | tf_op | source)
XLA Modules:
  0.0 268.4 jit_solution(16879019290114832526)
XLA Ops:
  0.0 1.4 collective-permute-start.1
  1.4 0.0 collective-permute-start.2
  1.4 0.5 collective-permute-start
  1.9 97.0 %vision.1.block = bf16[4,16,2176]{2,1,0:T(8,128)(2,1)} custom-call(bf16[64,1280]{1,0:T(8,128)(2,1)} %vit.1, s32[1,2]{1,0:T(1,128)} %ends.1, f32[1280]{0:T(1024)} %ln_gain.1, f32[1280]{0:T(1024)} %merger_gain.1, bf16[3,80,1280]{2,1,0:T(8,128)(2,1)} %bitcast.6, bf16[80,1280]{1,0:T(8,128)(2,1)} %w_proj.1, bf16[320,5120]{1,0:T(8,128)(2,1)} %bitcast.5, ...), custom_call_target="tpu_custom_call" | custom-call | tf_op jit(solution)/shard_map/vision/pallas_call | solution.py:481
  98.9 0.0 collective-permute-done.other_gain
  98.9 0.0 collective-permute-done.2.d_other
  99.0 0.0 collective-permute-done.1.w_other
  99.0 167.7 %feed_forward.1 = bf16[128,1024]{1,0:T(8,128)(2,1)} custom-call(bf16[4,16,2176]{2,1,0:T(8,128)(2,1)} %vision.1.block, s32[2048]{0:T(1024)} %slots.1, f32[1024]{0:T(1024)} %own_gain.1, f32[1024]{0:T(1024)} %collective-permute-done.other_gain, bf16[2,1848,1024]{2,1,0:T(8,128)(2,1)} %bitcast.4, bf16[2,1848,1024]{2,1,0:T(8,128)(2,1)} %collective-permute-done.1.w_other, ...), custom_call_target="tpu_custom_call" | custom-call | tf_op jit(solution)/shard_map/feed_forward/pallas_call | solution.py:829
  266.7 1.7 copy.14
Async XLA Ops:
  0.0 99.0 %collective-permute-start.1 = (bf16[2,1848,1024]{2,1,0:T(8,128)(2,1)}, bf16[2,1848,1024]{2,1,0:T(8,128)(2,1)}, u32[]{:S(2)}, u32[]{:S(2)}) collective-permute-start(bf16[2,1848,1024]{2,1,0:T(8,128)(2,1)} %bitcast.3), channel_id=1, source_target_pairs={{0,16},{16,0},{32,48},{48,32},{64,80},{80,64},{96,112},{112,96},{1... | collective-permute-start | bytes 22708232 | tf_op jit(solution)/shard_map/ppermute | solution.py:891
  1.4 97.6 %collective-permute-start.2 = (bf16[1848,1024]{1,0:T(8,128)(2,1)}, bf16[1848,1024]{1,0:T(8,128)(2,1)}, u32[]{:S(2)}, u32[]{:S(2)}) collective-permute-start(bf16[1848,1024]{1,0:T(8,128)(2,1)} %d_own.1), channel_id=1, source_target_pairs={{0,16},{16,0},{32,48},{48,32},{64,80},{80,64},{96,112},{112,96},{1... | collective-permute-start | bytes 11354120 | tf_op jit(solution)/shard_map/ppermute | solution.py:892
  1.4 97.5 %collective-permute-start = (f32[1024]{0:T(1024)}, f32[1024]{0:T(1024)}, u32[]{:S(2)}, u32[]{:S(2)}) collective-permute-start(f32[1024]{0:T(1024)} %own_gain.1), channel_id=1, source_target_pairs={{0,16},{16,0},{32,48},{48,32},{64,80},{80,64},{96,112},{112,96},{1... | collective-permute-start | bytes 12296 | tf_op jit(solution)/shard_map/ppermute | solution.py:893
